TPU v7x, 32 devices: a whole 2x2x4 slice. The times are simulated.
32 devices in a mesh: gx: 4 (over z), gy: 2 (over y), gz: 4 (over x, core).
Axes of the slice: x: 2, y: 2, z: 4, core: 2. Of those that a mesh axis runs over, the one named last changes fastest.
Arguments:
- start_disp: float32 [3, 32, 16, 512], P(None, 'gx', 'gy', 'gz'), may hold values from -2 to 2
- inertial: float32 [3, 32, 16, 512], P(None, 'gx', 'gy', 'gz'), may hold values from -1 to 1
- material: int32 [32, 16, 512], P('gx', 'gy', 'gz'), may hold values from 0 to 7
- pinned: int32 [32, 16, 512], P('gx', 'gy', 'gz'), may hold values 0 or 1
- stiffness: float32 [8], replicated, may hold values from 3 to 100
Outputs:
- displacement: float32 [3, 32, 16, 512], P(None, 'gx', 'gy', 'gz')
All inputs are finite; a program needn't handle non-finite values. No bound on the sum of `pinned` on one device may be relied on, other than what follows from the above.
Results may differ from a plain program's by a relative error of at most 0.0003.
Values sent between devices are 32-bit elements; how exact they have to be, the bound alone decides.
A program may use at most 64 MiB of HBM per device.

v0:
```python
import functools

import jax
import jax.numpy as jnp
from jax import lax
from jax.experimental import pallas as pl
from jax.experimental.pallas import tpu as pltpu
from jax.sharding import PartitionSpec as P

ITERS = 4
POLAR_STEPS = 6
MATS = 8

relax = 0.6
radius = 0.9
HALO = ITERS
SLOT = 2 * HALO
NARR = 8
GROUPS = 2
PAIRS = NARR // 2 // GROUPS
AXES = ("gx", "gy", "gz")


def loop(lo, hi, body, unroll=2):
    assert (hi - lo) % unroll == 0

    def group(k, _):
        body([lo + k * unroll + i for i in range(unroll)])
        return 0

    lax.fori_loop(0, (hi - lo) // unroll, group, 0)


def node_terms(u, uz, roll_y):
    zs, zd = uz + u, uz - u
    ys, yd = roll_y(zs), roll_y(zd)
    return zs + ys, ys - zs, zd + yd


def stretch(low, high):
    deform = []
    for c in range(3):
        dx = high[c][0] - low[c][0]
        dy = high[c][1] + low[c][1]
        dz = high[c][2] + low[c][2]
        row = [dx, dy, dz]
        row[c] = row[c] + 1.0
        deform.append(row)
    return deform


def stress(deform, w):
    total = None
    for c in range(3):
        for d in range(3):
            sq = deform[c][d] * deform[c][d]
            total = sq if total is None else total + sq
    inv = jnp.minimum(lax.rsqrt(total * (1.0 / 3.0)), 1.0) * (0.5**0.5)
    z = [[deform[c][d] * inv for d in range(3)] for c in range(3)]

    def polar(_, flat):
        z = [flat[3 * c : 3 * c + 3] for c in range(3)]
        s = {}
        for i in range(3):
            for j in range(i, 3):
                s[i, j] = z[0][i] * z[0][j] + z[1][i] * z[1][j] + z[2][i] * z[2][j]
        m = [1.5 - s[i, i] for i in range(3)]
        out = []
        for c in range(3):
            a, b, e = z[c]
            out.append(a * m[0] - b * s[0, 1] - e * s[0, 2])
            out.append(b * m[1] - a * s[0, 1] - e * s[1, 2])
            out.append(e * m[2] - a * s[0, 2] - b * s[1, 2])
        return tuple(out)

    flat = lax.fori_loop(
        0, POLAR_STEPS, polar, tuple(z[c][d] for c in range(3) for d in range(3)), unroll=True
    )
    return [w * (deform[k // 3][k % 3] - flat[k] * (2.0**0.5)) for k in range(9)]


def node_sums(before, here, roll_y):
    a = before[0] - here[0]
    b = before[1] + here[1]
    e = before[2] + here[2]
    g = (a - b) + roll_y(a + b)
    e = e + roll_y(e)
    return g - e, g + e


def advance(u, prev, inert, pin, rate, f, omega):
    target = u - rate * ((u - inert) + f)
    fresh = target if omega is None else omega * (target - prev) + prev
    return jnp.where(pin > 0.0, inert, fresh)


def kernel(
    counts, start, inertial, material, pinned, stiff, out,
    xe, sy, ry, ext, az, rz, prev, rate, terms, press, strip, sprev, srate, hz,
    send_sem, recv_sem,
):
    size_x, size_y, size_z = material.shape
    here = [lax.axis_index(a) for a in AXES]
    has = [[here[i] > 0, here[i] < counts[i] - 1] for i in range(3)]

    sub = lax.broadcasted_iota(jnp.int32, (size_y, size_z), 0)
    lane = lax.broadcasted_iota(jnp.int32, (size_y, size_z), 1)
    inside = ((sub < size_y - 1) | has[1][1]) & ((lane < size_z - 1) | has[2][1])
    quarter = [stiff[i] * 0.25 for i in range(MATS)]

    barrier = pltpu.get_barrier_semaphore()

    def peer(i, side):
        return {AXES[i]: here[i] + (1 if side else -1)}

    for i in range(3):
        for side in range(2):
            @pl.when(has[i][side])
            def _(i=i, side=side):
                pl.semaphore_signal(
                    barrier, inc=1, device_id=peer(i, side), device_id_type=pl.DeviceIdType.MESH
                )

    def faces(first, second):
        low = jnp.where(sub < HALO, first, pltpu.roll(second, HALO, 0))
        high = jnp.where(sub < HALO, pltpu.roll(first, HALO, 0), second)
        return low, high

    def pack_y(group, xs):
        done = [
            (p, x, faces(xe[2 * p, x], xe[2 * p + 1, x]))
            for x in xs for p in range(group * PAIRS, (group + 1) * PAIRS)
        ]
        for p, x, (low, high) in done:
            sy[0, p, x] = low
            sy[1, p, x] = high

    def own_planes(xs):
        done = []
        for x in xs:
            mat = material[x]
            w = jnp.zeros((size_y, size_z), jnp.float32)
            for index in range(MATS):
                w = jnp.where(mat == index, quarter[index], w)
            keep = inside & ((x < size_x - 1) | has[0][1])
            pins = pinned[x] > 0
            inert = [inertial[c, x] for c in range(3)]
            arrays = [jnp.where(pins, inert[c], start[c, x]) for c in range(3)] + inert
            arrays += [jnp.where(keep, w, 0.0), jnp.where(pins, 1.0, 0.0)]
            done.append((x + HALO, arrays))
        for x, arrays in done:
            for a in range(NARR):
                xe[a, x] = arrays[a]
            for p in range(NARR // 2):
                low, high = faces(arrays[2 * p], arrays[2 * p + 1])
                sy[0, p, x] = low
                sy[1, p, x] = high

    loop(0, size_x, own_planes, 4)

    def zero(ref, lo, n):
        def body(x, _):
            for a in range(ref.shape[0]):
                ref[a, x] = jnp.zeros(ref.shape[2:], jnp.float32)
            return 0
        lax.fori_loop(lo, lo + n, body, 0)

    top = HALO + size_x
    for side, lo in ((0, 0), (1, top)):
        @pl.when(jnp.logical_not(has[0][side]))
        def _(lo=lo):
            zero(xe, lo, HALO)
            for row in range(2):
                zero(ry.at[row, pl.ds(PAIRS, PAIRS)], lo, HALO)
    for side in range(2):
        @pl.when(jnp.logical_not(has[1][side]))
        def _(side=side):
            zero(ry.at[side], 0, top + HALO)

    n = 0
    for i in range(3):
        for side in range(2):
            n = n + has[i][side].astype(jnp.int32)
    pl.semaphore_wait(barrier, n)

    def remote(src, dst, k, i, side):
        return pltpu.make_async_remote_copy(
            src_ref=src, dst_ref=dst, send_sem=send_sem.at[k], recv_sem=recv_sem.at[k],
            device_id=peer(i, side), device_id_type=pl.DeviceIdType.MESH,
        )

    def x_copy(side, group):
        span = pl.ds(2 * PAIRS * group, 2 * PAIRS)
        src = xe.at[span, pl.ds(HALO if side == 0 else size_x, HALO)]
        dst = xe.at[span, pl.ds(top if side == 0 else 0, HALO)]
        return remote(src, dst, 2 * group + side, 0, side)

    def y_copy(side, part, group):
        lo, count = ((0, HALO), (HALO, size_x), (top, HALO))[part]
        span = pl.ds(PAIRS * group, PAIRS)
        return remote(
            sy.at[side, span, pl.ds(lo, count)], ry.at[1 - side, span, pl.ds(lo, count)],
            2 * GROUPS + (2 * part + side) * GROUPS + group, 1, side,
        )

    def corner(row, side):
        span = pl.ds(PAIRS, PAIRS)
        return remote(
            ry.at[row, span, pl.ds(HALO if side == 0 else size_x, HALO)],
            ry.at[row, span, pl.ds(top if side == 0 else 0, HALO)],
            8 * GROUPS + 2 + 2 * row + side, 0, side,
        )

    def z_copy(side):
        return remote(az, rz.at[1 - side], 8 * GROUPS + side, 2, side)

    def each(i, action):
        for side in range(2):
            @pl.when(has[i][side])
            def _(side=side):
                action(side)

    for group in range(GROUPS):
        each(0, lambda side: x_copy(side, group).start())
        each(1, lambda side: y_copy(side, 1, group).start())
    each(0, lambda side: x_copy(1 - side, 0).wait_recv())
    loop(0, HALO, functools.partial(pack_y, 0), HALO)
    loop(top, top + HALO, functools.partial(pack_y, 0), HALO)
    for part in (0, 2):
        each(1, lambda side: y_copy(side, part, 0).start())
    each(1, lambda row: y_copy(1 - row, 1, 1).wait_recv())
    each(1, lambda row: each(0, lambda side: corner(row, side).start()))

    wide = lax.broadcasted_iota(jnp.int32, (2 * HALO + size_y, size_z), 1)

    def fill(xs):
        done = []
        for x in xs:
            for p in range(NARR // 2):
                lo, hi = ry[0, p, x], ry[1, p, x]
                for q in range(2):
                    a = 2 * p + q
                    own = pltpu.roll(xe[a, x], HALO, 0)
                    lo_part = lo if q == 0 else pltpu.roll(lo, HALO, 0)
                    hi_part = hi if q == 1 else pltpu.roll(hi, HALO, 0)
                    done.append((
                        a, x, jnp.where(sub < HALO, lo_part, own),
                        jnp.where(sub < HALO, own, hi_part),
                    ))
        for a, x, low, high in done:
            ext[a, x, 0:size_y] = low
            ext[a, x, size_y : 2 * size_y] = high

    each(1, lambda row: y_copy(1 - row, 1, 0).wait_recv())
    loop(HALO, top, fill, 4)
    each(0, lambda side: x_copy(1 - side, 1).wait_recv())
    for part in (0, 2):
        each(1, lambda row: y_copy(1 - row, part, 0).wait_recv())
    each(1, lambda row: each(0, lambda side: corner(row, 1 - side).wait_recv()))
    loop(0, HALO, fill, HALO)
    loop(top, top + HALO, fill, HALO)

    planes = top + HALO

    def pack_z(arrays):
        packed = [jnp.zeros(wide.shape, jnp.float32) for _ in arrays]
        for x in range(planes):
            spot = (wide >= x * SLOT) & (wide < (x + 1) * SLOT)
            for k, a in enumerate(arrays):
                moved = pltpu.roll(ext[a, x], (x * SLOT + HALO) % size_z, 1)
                packed[k] = jnp.where(spot, moved, packed[k])
        for a, value in zip(arrays, packed):
            az[a] = value

    loop(0, NARR, pack_z, 4)
    each(2, lambda side: z_copy(side).start())

    rows = 2 * HALO + size_y
    up = lambda v: pltpu.roll(v, rows - 1, 0)
    down = lambda v: pltpu.roll(v, 1, 0)
    zup = lambda v: pltpu.roll(v, size_z - 1, 1)
    zdown = lambda v: pltpu.roll(v, 1, 1)

    def begin(xs):
        us = [(x, c, ext[c, x]) for x in xs for c in range(3)]
        for x, c, u in us:
            prev[c, x] = u

    def weigh(xs):
        sums = [ext[6, x - 1] + ext[6, x] for x in xs]
        sums = [w + down(w) for w in sums]
        for x, w in zip(xs, sums):
            rate[x] = w

    loop(0, planes, begin, 4)
    loop(1, planes - 1, weigh, (planes - 2) // 2)
    for side in range(2):
        @pl.when(jnp.logical_not(has[2][side]))
        def _(side=side):
            for a in range(NARR):
                rz[side, a] = jnp.zeros(wide.shape, jnp.float32)
    each(2, lambda side: z_copy(1 - side).wait_recv())

    early = lax.rem(wide, SLOT) < HALO
    for a in range(NARR):
        strip[0, a] = jnp.where(early, rz[0, a], az[a])
        strip[1, a] = jnp.where(early, az[a], rz[1, a])

    xup = lambda v: pltpu.roll(v, size_z - SLOT, 1)
    xdown = lambda v: pltpu.roll(v, SLOT, 1)

    def speed(total):
        return relax / (1.0 + 0.75 * total)

    for s in range(2):
        w = strip[s, 6]
        w = w + xdown(w)
        w = w + down(w)
        if s == 0:
            hz[0] = w
        srate[s] = speed(w + zdown(w))
        for c in range(3):
            sprev[s, c] = strip[s, c]

    first_lane = wide == 0
    last_lane = wide == size_z - 1

    def from_low(v, x):
        return pltpu.roll(v, size_z - HALO + 1 - SLOT * x, 1)

    def from_high(v, x):
        return pltpu.roll(v, size_z - 1 - HALO - SLOT * x, 1)

    def make_terms(x, c, u):
        uz = jnp.where(last_lane, from_high(strip[1, c], x), zup(u))
        return node_terms(u * 0.25, uz * 0.25, up)

    def put_terms(done):
        for x, c, three in done:
            for k in range(3):
                terms[x, 3 * c + k] = three[k]

    def setup(xs):
        us = [(x, c, ext[c, x]) for x in xs for c in range(3)]
        done = [(x, c, make_terms(x, c, u)) for x, c, u in us]
        put_terms(done)

    def setup_rate(xs):
        done = []
        for x in xs:
            w = rate[x]
            done.append(speed(w + jnp.where(first_lane, from_low(hz[0], x), zdown(w))))
        for x, r in zip(xs, done):
            rate[x] = r

    loop(0, planes, setup, 4)
    loop(1, planes - 1, setup_rate, (planes - 2) // 2)

    omega = None
    for step in range(ITERS):
        if step == 1:
            omega = 2.0 / (2.0 - radius * radius)
        elif step > 1:
            omega = 4.0 / (4.0 - radius * radius * omega)
        last = step == ITERS - 1

        def strips():
            done = []
            for s in range(2):
                low, high = [], []
                for c in range(3):
                    u = strip[s, c] * 0.25
                    t = node_terms(u, zup(u), up)
                    low.append(t)
                    high.append([xup(v) for v in t])
                p = stress(stretch(low, high), strip[s, 6])
                for c in range(3):
                    mine = p[3 * c : 3 * c + 3]
                    minus, plus = node_sums([xdown(v) for v in mine], mine, down)
                    u = strip[s, c]
                    fresh = advance(
                        u, sprev[s, c], strip[s, 3 + c], strip[s, 7], srate[s],
                        minus + zdown(plus), omega,
                    )
                    done.append((s, c, u, plus, fresh))
            for s, c, u, plus, fresh in done:
                if s == 0:
                    hz[c] = plus
                if not last:
                    sprev[s, c] = u
                    strip[s, c] = fresh

        def voxels(x, _):
            low = [[terms[x, 3 * c + k] for k in range(3)] for c in range(3)]
            high = [[terms[x + 1, 3 * c + k] for k in range(3)] for c in range(3)]
            p = stress(stretch(low, high), ext[6, x])
            for k in range(9):
                press[x, k] = p[k]
            return 0

        def nodes(xs):
            done = []
            for x in xs:
                for c in range(3):
                    minus, plus = node_sums(
                        [press[x - 1, 3 * c + k] for k in range(3)],
                        [press[x, 3 * c + k] for k in range(3)],
                        down,
                    )
                    f = minus + jnp.where(first_lane, from_low(hz[c], x), zdown(plus))
                    u = ext[c, x]
                    fresh = advance(u, prev[c, x], ext[3 + c, x], ext[7, x], rate[x], f, omega)
                    done.append((x, c, u, fresh))
            if last:
                for x, c, _, fresh in done:
                    out[c, x - HALO] = fresh[HALO : HALO + size_y]
                return
            later = [(x, c, make_terms(x, c, fresh)) for x, c, _, fresh in done]
            for x, c, u, fresh in done:
                prev[c, x] = u
                ext[c, x] = fresh
            put_terms(later)

        strips()
        lax.fori_loop(step, planes - 1 - step, voxels, 0)
        loop(step + 1, planes - 1 - step, nodes)

    for group in range(GROUPS):
        each(0, lambda side: x_copy(side, group).wait_send())
        each(1, lambda side: y_copy(side, 1, group).wait_send())
    for part in (0, 2):
        each(1, lambda side: y_copy(side, part, 0).wait_send())
    each(1, lambda row: each(0, lambda side: corner(row, side).wait_send()))
    each(2, lambda side: z_copy(side).wait_send())


def per_device(counts, start_disp, inertial, material, pinned, stiffness):
    size_x, size_y, size_z = material.shape
    planes, rows = size_x + 2 * HALO, size_y + 2 * HALO
    assert planes * SLOT == size_z and size_y == 2 * HALO
    vmem = pl.BlockSpec(memory_space=pltpu.VMEM)
    f32 = lambda *shape: pltpu.VMEM(shape, jnp.float32)
    return pl.pallas_call(
        functools.partial(kernel, counts),
        out_shape=jax.ShapeDtypeStruct(start_disp.shape, jnp.float32),
        in_specs=[vmem, vmem, vmem, vmem, pl.BlockSpec(memory_space=pltpu.SMEM)],
        out_specs=vmem,
        scratch_shapes=[
            f32(NARR, planes, size_y, size_z),
            f32(2, NARR // 2, planes, size_y, size_z),
            f32(2, NARR // 2, planes, size_y, size_z),
            f32(NARR, planes, rows, size_z),
            f32(NARR, rows, size_z),
            f32(2, NARR, rows, size_z),
            f32(3, planes, rows, size_z),
            f32(planes, rows, size_z),
            f32(planes, 9, rows, size_z),
            f32(planes, 9, rows, size_z),
            f32(2, NARR, rows, size_z),
            f32(2, 3, rows, size_z),
            f32(2, rows, size_z),
            f32(3, rows, size_z),
            pltpu.SemaphoreType.DMA((8 * GROUPS + 6,)),
            pltpu.SemaphoreType.DMA((8 * GROUPS + 6,)),
        ],
        compiler_params=pltpu.CompilerParams(collective_id=0, has_side_effects=True),
    )(start_disp, inertial, material, pinned, stiffness)


def solution(mesh):
    placed = (
        P(None, "gx", "gy", "gz"),
        P(None, "gx", "gy", "gz"),
        P("gx", "gy", "gz"),
        P("gx", "gy", "gz"),
        P(),
    )
    counts = tuple(mesh.shape[a] for a in AXES)
    return jax.shard_map(
        functools.partial(per_device, counts), mesh=mesh, in_specs=placed,
        out_specs=P(None, "gx", "gy", "gz"), check_vma=False,
    )
```

profile of v0, /device:TPU:1, one launch (start us, length us, event | category | flops | bytes accessed | tf_op | source)
XLA Modules:
  0.0 32.7 jit_solution(16575325728091253471)
XLA Ops:
  0.0 31.1 %shard_map.55 = f32[3,8,8,128]{3,2,1,0:T(8,128)} custom-call(f32[3,8,8,128]{3,2,1,0:T(8,128)} %start.1, f32[3,8,8,128]{3,2,1,0:T(8,128)} %inertial.1, s32[8,8,128]{2,1,0:T(8,128)} %material.1, s32[8,8,128]{2,1,0:T(8,128)} %pinned.1, f32[8]{0:T(128)} %stiff.1), custom_call_target="tpu_custom_call" | custom-call | tf_op jit(solution)/shard_map/pallas_call | solution.py:443
  31.1 1.5 %copy.7 = f32[3,8,8,128]{3,2,1,0:T(8,128)} copy(f32[3,8,8,128]{3,2,1,0:T(8,128)} %shard_map.55) | data formatting | bytes 196608
where the time goes:
time: 32.8 us; the launch traced here: 32.7 us
  Pallas kernels  31.1 us (95%)
  local copies, waits for them, and re-layouts  1.54 us (5%)
    pallas_call x1, Pallas kernels, per_device(): pl.pallas_call(functools.partial(kernel, counts), out_shape=jax.ShapeDtyp...  31.1 us
    unnamed x1, local copies, waits for them, and re-layouts  1.54 us

commit v1 on v0

--- a/solution.py
+++ b/solution.py
@@ -49,34 +49,76 @@
     return deform
 
 
+COSINE = (
+    1.00000005, 1.15469445, -0.222086479, 0.105738212,
+    -0.0606261262, 0.0323189784, -0.0123398994, 0.00230085802,
+)
+
+
 def stress(deform, w):
-    total = None
-    for c in range(3):
-        for d in range(3):
-            sq = deform[c][d] * deform[c][d]
-            total = sq if total is None else total + sq
-    inv = jnp.minimum(lax.rsqrt(total * (1.0 / 3.0)), 1.0) * (0.5**0.5)
-    z = [[deform[c][d] * inv for d in range(3)] for c in range(3)]
-
-    def polar(_, flat):
-        z = [flat[3 * c : 3 * c + 3] for c in range(3)]
-        s = {}
-        for i in range(3):
-            for j in range(i, 3):
-                s[i, j] = z[0][i] * z[0][j] + z[1][i] * z[1][j] + z[2][i] * z[2][j]
-        m = [1.5 - s[i, i] for i in range(3)]
-        out = []
-        for c in range(3):
-            a, b, e = z[c]
-            out.append(a * m[0] - b * s[0, 1] - e * s[0, 2])
-            out.append(b * m[1] - a * s[0, 1] - e * s[1, 2])
-            out.append(e * m[2] - a * s[0, 2] - b * s[1, 2])
-        return tuple(out)
-
-    flat = lax.fori_loop(
-        0, POLAR_STEPS, polar, tuple(z[c][d] for c in range(3) for d in range(3)), unroll=True
-    )
-    return [w * (deform[k // 3][k % 3] - flat[k] * (2.0**0.5)) for k in range(9)]
+    f = deform
+    s = {}
+    for i in range(3):
+        for j in range(i, 3):
+            s[i, j] = f[0][i] * f[0][j] + f[1][i] * f[1][j] + f[2][i] * f[2][j]
+    mean = (s[0, 0] + s[1, 1] + s[2, 2]) * (1.0 / 3.0)
+    inv = jnp.minimum(lax.rsqrt(mean), 1.0)
+    k11, k22, k33 = (s[i, i] - mean for i in range(3))
+    k12, k13, k23 = s[0, 1], s[0, 2], s[1, 2]
+    a11, a12, a13, a23 = k11 * k11, k12 * k12, k13 * k13, k23 * k23
+    b23, c23 = k22 * k33, k12 * k13
+    spread = a11 - b23 + a12 + (a13 + a23)
+    spread = jnp.maximum(spread * (1.0 / 3.0), 1e-30)
+    rp = lax.rsqrt(spread)
+    rp2 = rp * rp
+    det = k11 * (b23 - a23) - k22 * a13 + ((c23 + c23) * k23 - k33 * a12)
+    half = 0.5 + 0.25 * (det * rp * rp2)
+    half = jnp.minimum(jnp.maximum(half, 1e-12), 1.0)
+    root = half * lax.rsqrt(half)
+    e = COSINE[-1]
+    for a in COSINE[-2::-1]:
+        e = e * root + a
+    t2 = jnp.maximum(3.0 - 0.75 * (e * e), 1e-12)
+    y = lax.rsqrt(t2)
+    t = t2 * y
+    e2 = 0.5 * e
+    e3 = e + e2
+    x2, x3 = t - e2, t + e2
+    r12 = 1.0 / jnp.maximum(e3 - t, 1e-6)
+    r13 = 1.0 / (e3 + t)
+    r23 = 0.5 * y
+    scale = 0.5 * (inv * inv)
+    p = spread * rp * scale
+    mean = mean * scale
+    inv = inv * w
+    qs = []
+    for h in (mean + p * e, mean + p * x2, mean - p * x3):
+        m = 1.5 - h
+        q = inv * m
+        for _ in range(POLAR_STEPS - 1):
+            h = h * (m * m)
+            m = 1.5 - h
+            q = q * m
+        qs.append(q)
+    q12 = (qs[0] - qs[1]) * r12
+    q23 = (qs[1] - qs[2]) * r23
+    c2 = (q12 - q23) * r13
+    c0 = (w - qs[0]) + (q12 * e - c2 * (e * x2))
+    c1 = (c2 * x3 - q12) * rp
+    c2 = c2 * rp2
+    g = {
+        (0, 0): (c0 + c1 * k11) - c2 * (a11 + (a12 + a13)),
+        (1, 1): (c0 + c1 * k22) - c2 * (k22 * k22 + (a12 + a23)),
+        (2, 2): (c0 + c1 * k33) - c2 * (k33 * k33 + (a13 + a23)),
+        (0, 1): c1 * k12 - c2 * (k13 * k23 - k12 * k33),
+        (0, 2): c1 * k13 - c2 * (k12 * k23 - k13 * k22),
+        (1, 2): c1 * k23 - c2 * (c23 - k23 * k11),
+    }
+    pick = lambda i, j: g[min(i, j), max(i, j)]
+    return [
+        f[c][0] * pick(0, d) + f[c][1] * pick(1, d) + f[c][2] * pick(2, d)
+        for c in range(3) for d in range(3)
+    ]
 
 
 def node_sums(before, here, roll_y):

time: 32.8 us -> 30.5 us (0.930)
  Pallas kernels: 31.1 us -> 28.7 us
    pallas_call x1, Pallas kernels: 31.1 us -> 28.7 us  [per_device(): pl.pallas_call(functools.partial(kernel, counts), out_shape=jax.ShapeDtyp...]
where the time goes in v1:
time: 30.5 us; the launch traced here: 30.3 us
  Pallas kernels  28.7 us (94%)
  local copies, waits for them, and re-layouts  1.54 us (5%)
    pallas_call x1, Pallas kernels, per_device(): pl.pallas_call(functools.partial(kernel, counts), out_shape=jax.ShapeDtyp...  28.7 us
    unnamed x1, local copies, waits for them, and re-layouts  1.54 us

profile of v1, /device:TPU:1, one launch (start us, length us, event | category | flops | bytes accessed | tf_op | source)
XLA Modules:
  0.0 30.3 jit_solution(377539783489335930)
XLA Ops:
  0.0 28.7 %shard_map.55 = f32[3,8,8,128]{3,2,1,0:T(8,128)} custom-call(f32[3,8,8,128]{3,2,1,0:T(8,128)} %start.1, f32[3,8,8,128]{3,2,1,0:T(8,128)} %inertial.1, s32[8,8,128]{2,1,0:T(8,128)} %material.1, s32[8,8,128]{2,1,0:T(8,128)} %pinned.1, f32[8]{0:T(128)} %stiff.1), custom_call_target="tpu_custom_call" | custom-call | tf_op jit(solution)/shard_map/pallas_call | solution.py:485
  28.7 1.5 %copy.7 = f32[3,8,8,128]{3,2,1,0:T(8,128)} copy(f32[3,8,8,128]{3,2,1,0:T(8,128)} %shard_map.55) | data formatting | bytes 196608

commit v2 on v1

v2 whole, which is shorter than its diff:
```python
import functools
import itertools

import jax
import jax.numpy as jnp
from jax import lax
from jax.experimental import pallas as pl
from jax.experimental.pallas import tpu as pltpu
from jax.sharding import PartitionSpec as P

ITERS = 4
POLAR_STEPS = 6
MATS = 8

relax = 0.6
radius = 0.9
HALO = ITERS
SLOT = 2 * HALO
NARR = 8
SPAN = NARR // 2
WEIGHT, INERT, PIN = 3, 4, 7
AXES = ("gx", "gy", "gz")
AROUND = tuple(o for o in itertools.product((-1, 0, 1), repeat=3) if any(o))
DIAGONAL = tuple(itertools.product((-1, 1), repeat=2))
FACES = len(AROUND)
CORNERS = FACES + 8
COPIES = CORNERS + 8


def loop(lo, hi, body, unroll=2):
    assert (hi - lo) % unroll == 0

    def group(k, _):
        body([lo + k * unroll + i for i in range(unroll)])
        return 0

    lax.fori_loop(0, (hi - lo) // unroll, group, 0)


def node_terms(u, uz, roll_y):
    zs, zd = uz + u, uz - u
    ys, yd = roll_y(zs), roll_y(zd)
    return zs + ys, ys - zs, zd + yd


def stretch(low, high):
    deform = []
    for c in range(3):
        dx = high[c][0] - low[c][0]
        dy = high[c][1] + low[c][1]
        dz = high[c][2] + low[c][2]
        row = [dx, dy, dz]
        row[c] = row[c] + 1.0
        deform.append(row)
    return deform


COSINE = (
    1.00000005, 1.15469445, -0.222086479, 0.105738212,
    -0.0606261262, 0.0323189784, -0.0123398994, 0.00230085802,
)


def stress(deform, w):
    f = deform
    s = {}
    for i in range(3):
        for j in range(i, 3):
            s[i, j] = f[0][i] * f[0][j] + f[1][i] * f[1][j] + f[2][i] * f[2][j]
    mean = (s[0, 0] + s[1, 1] + s[2, 2]) * (1.0 / 3.0)
    inv = jnp.minimum(lax.rsqrt(mean), 1.0)
    k11, k22, k33 = (s[i, i] - mean for i in range(3))
    k12, k13, k23 = s[0, 1], s[0, 2], s[1, 2]
    a11, a12, a13, a23 = k11 * k11, k12 * k12, k13 * k13, k23 * k23
    b23, c23 = k22 * k33, k12 * k13
    spread = a11 - b23 + a12 + (a13 + a23)
    spread = jnp.maximum(spread * (1.0 / 3.0), 1e-30)
    rp = lax.rsqrt(spread)
    rp2 = rp * rp
    det = k11 * (b23 - a23) - k22 * a13 + ((c23 + c23) * k23 - k33 * a12)
    half = 0.5 + 0.25 * (det * rp * rp2)
    half = jnp.minimum(jnp.maximum(half, 1e-12), 1.0)
    root = half * lax.rsqrt(half)
    e = COSINE[-1]
    for a in COSINE[-2::-1]:
        e = e * root + a
    t2 = jnp.maximum(3.0 - 0.75 * (e * e), 1e-12)
    y = lax.rsqrt(t2)
    t = t2 * y
    e2 = 0.5 * e
    e3 = e + e2
    x2, x3 = t - e2, t + e2
    r12 = 1.0 / jnp.maximum(e3 - t, 1e-6)
    r13 = 1.0 / (e3 + t)
    r23 = 0.5 * y
    scale = 0.5 * (inv * inv)
    p = spread * rp * scale
    mean = mean * scale
    inv = inv * w
    qs = []
    for h in (mean + p * e, mean + p * x2, mean - p * x3):
        m = 1.5 - h
        q = inv * m
        for _ in range(POLAR_STEPS - 1):
            h = h * (m * m)
            m = 1.5 - h
            q = q * m
        qs.append(q)
    q12 = (qs[0] - qs[1]) * r12
    q23 = (qs[1] - qs[2]) * r23
    c2 = (q12 - q23) * r13
    c0 = (w - qs[0]) + (q12 * e - c2 * (e * x2))
    c1 = (c2 * x3 - q12) * rp
    c2 = c2 * rp2
    g = {
        (0, 0): (c0 + c1 * k11) - c2 * (a11 + (a12 + a13)),
        (1, 1): (c0 + c1 * k22) - c2 * (k22 * k22 + (a12 + a23)),
        (2, 2): (c0 + c1 * k33) - c2 * (k33 * k33 + (a13 + a23)),
        (0, 1): c1 * k12 - c2 * (k13 * k23 - k12 * k33),
        (0, 2): c1 * k13 - c2 * (k12 * k23 - k13 * k22),
        (1, 2): c1 * k23 - c2 * (c23 - k23 * k11),
    }
    pick = lambda i, j: g[min(i, j), max(i, j)]
    return [
        f[c][0] * pick(0, d) + f[c][1] * pick(1, d) + f[c][2] * pick(2, d)
        for c in range(3) for d in range(3)
    ]


def node_sums(before, here, roll_y):
    a = before[0] - here[0]
    b = before[1] + here[1]
    e = before[2] + here[2]
    g = (a - b) + roll_y(a + b)
    e = e + roll_y(e)
    return g - e, g + e


def advance(u, prev, inert, rate, f, omega):
    target = u - rate * ((u - inert) + f)
    return target if omega is None else omega * (target - prev()) + prev()


def kernel(
    counts, start, inertial, material, pinned, stiff, out,
    first, mat, pins, ext, pk, rz, strip, sprev, srate, zin, prev, rate, terms, press, done,
    send_sem, recv_sem, load_sem,
):
    size_x, size_y, size_z = material.shape
    top = HALO + size_x
    planes = top + HALO
    rows = 2 * size_y
    own_y, own_x = pl.ds(0, size_y), pl.ds(HALO, size_x)
    here = [lax.axis_index(a) for a in AXES]
    has = [{-1: here[i] > 0, 1: here[i] < counts[i] - 1} for i in range(3)]

    loads = [
        pltpu.make_async_copy(pinned, pins, load_sem.at[0]),
        pltpu.make_async_copy(material, mat, load_sem.at[1]),
        pltpu.make_async_copy(inertial, ext.at[pl.ds(INERT, 3), own_x, own_y], load_sem.at[2]),
        pltpu.make_async_copy(start, first, load_sem.at[3]),
    ]
    for copy in loads:
        copy.start()

    def exists(offset):
        found = None
        for i, o in enumerate(offset):
            if o:
                found = has[i][o] if found is None else found & has[i][o]
        return found

    def peer(offset):
        return {AXES[i]: here[i] + o for i, o in enumerate(offset) if o}

    def back(offset):
        return tuple(-o for o in offset)

    blank = jnp.zeros((size_y, size_z), jnp.float32)

    def clear(xs, spots):
        for x in xs:
            for a in range(NARR):
                for spot in spots:
                    ext[a, x, spot * size_y : (spot + 1) * size_y] = blank

    for z in range(3):
        for group in range(2):
            for g in range(4):
                for spot in range(2):
                    if (z, spot) != (1, 0) or g in (0, 3):
                        rz[z, group, g, spot * size_y : (spot + 1) * size_y] = blank
    loop(0, HALO, lambda xs: clear(xs, (0, 1)), 2)
    loop(HALO, top, lambda xs: clear(xs, (1,)), 4)
    loop(top, planes, lambda xs: clear(xs, (0, 1)), 2)

    barrier = pltpu.get_barrier_semaphore()
    for offset in AROUND:
        @pl.when(exists(offset))
        def _(offset=offset):
            pl.semaphore_signal(
                barrier, inc=1, device_id=peer(offset), device_id_type=pl.DeviceIdType.MESH
            )

    sub = lax.broadcasted_iota(jnp.int32, (size_y, size_z), 0)
    lane = lax.broadcasted_iota(jnp.int32, (size_y, size_z), 1)
    inside = ((sub < size_y - 1) | has[1][1]) & ((lane < size_z - 1) | has[2][1])
    quarter = [stiff[i] * 0.25 for i in range(MATS)]
    block = size_z // 4

    for copy in loads:
        copy.wait()

    for h in range(2):
        packed = [blank, blank]
        for i in range(HALO):
            x = HALO * h + i
            m = mat[x]
            w = jnp.zeros((size_y, size_z), jnp.float32)
            for index in range(MATS):
                w = jnp.where(m == index, quarter[index], w)
            keep = inside if x < size_x - 1 else inside & has[0][1]
            pin = pins[x] > 0
            inert = [ext[INERT + c, x + HALO, 0:size_y] for c in range(3)]
            arrays = [jnp.where(pin, inert[c], first[c, x]) for c in range(3)]
            arrays += [jnp.where(keep, w, 0.0)] + inert + [jnp.where(pin, 1.0, 0.0)]
            for a in (0, 1, 2, WEIGHT, PIN):
                ext[a, x + HALO, 0:size_y] = arrays[a]
            for a in range(NARR):
                spot = block * (a % SPAN) + SLOT * i
                moved = pltpu.roll(arrays[a], (spot + HALO) % size_z, 1)
                mine = (lane >= spot) & (lane < spot + SLOT)
                packed[a // SPAN] = jnp.where(mine, moved, packed[a // SPAN])
        for group in range(2):
            pk[group, h] = packed[group]
            rz[1, group, 1 + h, 0:size_y] = packed[group]

    def remote(src, dst, k, offset):
        return pltpu.make_async_remote_copy(
            src_ref=src, dst_ref=dst, send_sem=send_sem.at[k], recv_sem=recv_sem.at[k],
            device_id=peer(offset), device_id_type=pl.DeviceIdType.MESH,
        )

    def row_spans(dy, depth):
        if dy == 0:
            return own_y, own_y
        if dy > 0:
            return pl.ds(size_y - depth, depth), pl.ds(rows - depth, depth)
        return pl.ds(0, depth), pl.ds(size_y, depth)

    def plane_spans(dx, depth):
        if dx == 0:
            return own_x, own_x
        if dx > 0:
            return pl.ds(top - depth, depth), pl.ds(HALO - depth, depth)
        return pl.ds(HALO, depth), pl.ds(top, depth)

    def piece(k):
        dx, dy, dz = AROUND[k]
        parts = {0: (pl.ds(0, 2), pl.ds(1, 2)), 1: (pl.ds(1, 1), pl.ds(0, 1)), -1: (pl.ds(0, 1), pl.ds(3, 1))}
        h, g = parts[dx]
        r, to = row_spans(dy, HALO)
        return remote(pk.at[:, h, r], rz.at[1 - dz, :, g, to], k, AROUND[k])

    depths = (HALO, HALO - 1)
    sides = (-1, 1)

    def face(axis, side, group):
        offset = tuple(side if i == axis else 0 for i in range(3))
        x, x_to = plane_spans(offset[0], depths[group])
        y, y_to = row_spans(offset[1], depths[group])
        span = pl.ds(SPAN * group, SPAN)
        k = FACES + 4 * axis + 2 * group + (side > 0)
        return remote(ext.at[span, x, y], ext.at[span, x_to, y_to], k, offset)

    def corner(dx, dy, group):
        x, x_to = plane_spans(dx, depths[group])
        y, y_to = row_spans(dy, depths[group])
        span = pl.ds(SPAN * group, SPAN)
        k = CORNERS + 4 * group + 2 * (dx > 0) + (dy > 0)
        if group == 0:
            return remote(ext.at[span, x, y_to], ext.at[span, x_to, y_to], k, (dx, 0, 0))
        return remote(ext.at[span, x, y], ext.at[span, x_to, y_to], k, (dx, dy, 0))

    def when(condition, action):
        pl.when(condition)(action)

    def send_face(axis, group):
        for side in sides:
            when(has[axis][side], lambda side=side: face(axis, side, group).start())

    def get_face(axis, group):
        for side in sides:
            when(has[axis][-side], lambda side=side: face(axis, side, group).wait_recv())

    def sent_face(axis, group):
        for side in sides:
            when(has[axis][side], lambda side=side: face(axis, side, group).wait_send())

    n = 1
    for i in range(3):
        n = n * (1 + has[i][-1].astype(jnp.int32) + has[i][1].astype(jnp.int32))
    pl.semaphore_wait(barrier, n - 1)

    send_face(1, 0)
    send_face(0, 0)
    for k, offset in enumerate(AROUND):
        when(exists(offset), lambda k=k: piece(k).start())
    send_face(1, 1)
    send_face(0, 1)
    for dx, dy in DIAGONAL:
        when(exists((dx, dy)), lambda dx=dx, dy=dy: corner(dx, dy, 1).start())

    get_face(1, 0)
    for dx, dy in DIAGONAL:
        when(has[0][dx] & has[1][-dy], lambda dx=dx, dy=dy: corner(dx, dy, 0).start())

    wide = lax.broadcasted_iota(jnp.int32, (rows, size_z), 1)
    edge = (wide == 0) | (wide == size_z - 1)
    up = lambda v: pltpu.roll(v, rows - 1, 0)
    down = lambda v: pltpu.roll(v, 1, 0)
    zup = lambda v: pltpu.roll(v, size_z - 1, 1)
    zdown = lambda v: pltpu.roll(v, 1, 1)
    xup = lambda v: pltpu.roll(v, size_z - SLOT, 1)
    xdown = lambda v: pltpu.roll(v, SLOT, 1)

    def make_terms(u):
        u = u * 0.25
        return node_terms(u, zup(u), up)

    def setup(xs):
        made = [(x, c, make_terms(ext[c, x])) for x in xs for c in range(3)]
        for x, c, three in made:
            for k in range(3):
                terms[x, 3 * c + k] = three[k]

    def voxels(xs):
        made = []
        for x in xs:
            low = [[terms[x, 3 * c + k] for k in range(3)] for c in range(3)]
            high = [[terms[x + 1, 3 * c + k] for k in range(3)] for c in range(3)]
            made.append((x, stress(stretch(low, high), ext[WEIGHT, x])))
        for x, p in made:
            for k in range(9):
                press[x, k] = p[k]

    def all_voxels(lo, hi):
        if (hi - lo) % 2:
            voxels([hi - 3, hi - 2, hi - 1])
            hi = hi - 3
        loop(lo, hi, voxels, 2)

    loop(HALO, top, setup, 4)
    all_voxels(HALO, top - 1)

    for k, offset in enumerate(AROUND):
        when(exists(back(offset)), lambda k=k: piece(k).wait_recv())

    late = lax.rem(wide, SLOT) >= HALO
    for group in range(2):
        for s in range(2):
            parts = [
                jnp.where(late, rz[s + 1, group, g], rz[s, group, g]) for g in range(4)
            ]
            for j in range(SPAN):
                value = None
                for g in range(4):
                    moved = parts[g]
                    if g != j:
                        moved = pltpu.roll(moved, (block * (g - j)) % size_z, 1)
                    value = moved if g == 0 else jnp.where(wide >= block * g, moved, value)
                strip[s, SPAN * group + j] = value

    def speed(total, pin):
        return jnp.where(pin > 0.0, 0.0, relax / (1.0 + 0.75 * total))

    for s in range(2):
        w = strip[s, WEIGHT]
        w = w + xdown(w)
        w = w + down(w)
        srate[s] = speed(w + zdown(w), strip[s, PIN])

    joint = lax.rem(wide, SLOT) == HALO

    def bring(low, high):
        return pltpu.roll(jnp.where(joint, low, high), size_z - HALO, 1)

    omegas = [None, 2.0 / (2.0 - radius * radius)]
    while len(omegas) < ITERS:
        omegas.append(4.0 / (4.0 - radius * radius * omegas[-1]))

    def strips(step):
        made = []
        for s in range(2):
            low, high = [], []
            for c in range(3):
                t = make_terms(strip[s, c])
                low.append(t)
                high.append([xup(v) for v in t])
            made.append(stress(stretch(low, high), strip[s, WEIGHT]))
        for c in range(3):
            sums, fresh = [], []
            for s in range(2):
                mine = made[s][3 * c : 3 * c + 3]
                minus, plus = node_sums([xdown(v) for v in mine], mine, down)
                sums.append((minus, plus))
                if step < ITERS - 1:
                    u = strip[s, c]
                    fresh.append(advance(
                        u, lambda: sprev[s, c], strip[s, INERT + c], srate[s],
                        minus + zdown(plus), omegas[step],
                    ))
                    sprev[s, c] = u
                    strip[s, c] = fresh[s]
            if step < ITERS - 1:
                zin[step, c] = bring(*fresh)
            else:
                zin[step, c] = bring(zdown(sums[0][1]), sums[1][0])

    for step in range(ITERS):
        strips(step)

    get_face(0, 0)
    for dx, dy in DIAGONAL:
        when(has[0][-dx] & has[1][-dy], lambda dx=dx, dy=dy: corner(dx, dy, 0).wait_recv())
    loop(0, HALO, setup, 4)
    loop(top, planes, setup, 4)
    all_voxels(0, HALO)
    all_voxels(top - 1, planes - 1)

    get_face(1, 1)
    get_face(0, 1)
    for dx, dy in DIAGONAL:
        when(has[0][-dx] & has[1][-dy], lambda dx=dx, dy=dy: corner(dx, dy, 1).wait_recv())

    for axis in range(2):
        sent_face(axis, 0)
    for dx, dy in DIAGONAL:
        when(has[0][dx] & has[1][-dy], lambda dx=dx, dy=dy: corner(dx, dy, 0).wait_send())

    def place(value, x):
        return pltpu.roll(value, size_z - SLOT * x, 1)

    def weigh(xs):
        made = []
        for x in xs:
            w = ext[WEIGHT, x - 1] + ext[WEIGHT, x]
            w = w + down(w)
            value = speed(w + zdown(w), ext[PIN, x])
            low = pltpu.roll(srate[0], size_z - HALO - SLOT * x + size_z, 1)
            made.append((x, jnp.where(wide == 0, low, value)))
        for x, value in made:
            rate[x] = value

    loop(1, planes - 1, weigh, (planes - 2) // 2)

    def nodes(step, xs):
        made = []
        last = step == ITERS - 1
        for x in xs:
            r = rate[x]
            for c in range(3):
                minus, plus = node_sums(
                    [press[x - 1, 3 * c + k] for k in range(3)],
                    [press[x, 3 * c + k] for k in range(3)],
                    down,
                )
                plus = zdown(plus)
                beside = place(zin[step, c], x)
                if last:
                    minus = jnp.where(wide == size_z - 1, beside, minus)
                    plus = jnp.where(wide == 0, beside, plus)
                u = ext[c, x]
                fresh = advance(
                    u, lambda: prev[c, x], ext[INERT + c, x], r, minus + plus, omegas[step]
                )
                if not last:
                    fresh = jnp.where(edge, beside, fresh)
                made.append((x, c, u, fresh))
        if last:
            for x, c, _, fresh in made:
                done[c, x - HALO] = fresh[0:size_y]
            return
        later = [(x, c, make_terms(fresh)) for x, c, _, fresh in made]
        for x, c, u, fresh in made:
            prev[c, x] = u
            ext[c, x] = fresh
        for x, c, three in later:
            for k in range(3):
                terms[x, 3 * c + k] = three[k]

    for step in range(ITERS):
        if step:
            all_voxels(step, planes - 1 - step)
        if step < ITERS - 1:
            loop(step + 1, planes - 1 - step, functools.partial(nodes, step))

    stores = []
    for h in range(2):
        loop(HALO * (h + 1), HALO * (h + 2), functools.partial(nodes, ITERS - 1), 4)
        span = pl.ds(HALO * h, HALO)
        stores.append(pltpu.make_async_copy(done.at[:, span], out.at[:, span], load_sem.at[h]))
        stores[h].start()

    for axis in range(2):
        sent_face(axis, 1)
    for k, offset in enumerate(AROUND):
        when(exists(offset), lambda k=k: piece(k).wait_send())
    for dx, dy in DIAGONAL:
        when(exists((dx, dy)), lambda dx=dx, dy=dy: corner(dx, dy, 1).wait_send())
    for copy in stores:
        copy.wait()


def per_device(counts, start_disp, inertial, material, pinned, stiffness):
    size_x, size_y, size_z = material.shape
    planes, rows = size_x + 2 * HALO, 2 * size_y
    assert planes * SLOT == size_z and size_y == 2 * HALO and size_x == 2 * HALO
    hbm = pl.BlockSpec(memory_space=pl.ANY)
    f32 = lambda *shape: pltpu.VMEM(shape, jnp.float32)
    i32 = lambda *shape: pltpu.VMEM(shape, jnp.int32)
    return pl.pallas_call(
        functools.partial(kernel, counts),
        out_shape=jax.ShapeDtypeStruct(start_disp.shape, jnp.float32),
        in_specs=[hbm, hbm, hbm, hbm, pl.BlockSpec(memory_space=pltpu.SMEM)],
        out_specs=hbm,
        scratch_shapes=[
            f32(3, size_x, size_y, size_z),
            i32(size_x, size_y, size_z),
            i32(size_x, size_y, size_z),
            f32(NARR, planes, rows, size_z),
            f32(2, 2, size_y, size_z),
            f32(3, 2, 4, rows, size_z),
            f32(2, NARR, rows, size_z),
            f32(2, 3, rows, size_z),
            f32(2, rows, size_z),
            f32(ITERS, 3, rows, size_z),
            f32(3, planes, rows, size_z),
            f32(planes, rows, size_z),
            f32(planes, 9, rows, size_z),
            f32(planes, 9, rows, size_z),
            f32(3, size_x, size_y, size_z),
            pltpu.SemaphoreType.DMA((COPIES,)),
            pltpu.SemaphoreType.DMA((COPIES,)),
            pltpu.SemaphoreType.DMA((4,)),
        ],
        compiler_params=pltpu.CompilerParams(collective_id=0, has_side_effects=True),
    )(start_disp, inertial, material, pinned, stiffness)


def solution(mesh):
    placed = (
        P(None, "gx", "gy", "gz"),
        P(None, "gx", "gy", "gz"),
        P("gx", "gy", "gz"),
        P("gx", "gy", "gz"),
        P(),
    )
    counts = tuple(mesh.shape[a] for a in AXES)
    return jax.shard_map(
        functools.partial(per_device, counts), mesh=mesh, in_specs=placed,
        out_specs=P(None, "gx", "gy", "gz"), check_vma=False,
    )
```

time: 30.5 us -> 22.6 us (0.74)
  Pallas kernels: 28.7 us -> 20.6 us
    pallas_call x1, Pallas kernels: 28.7 us -> 20.6 us  [per_device(): pl.pallas_call(functools.partial(kernel, counts), out_shape=jax.ShapeDtyp...]
where the time goes in v2:
time: 22.6 us; the launch traced here: 22.2 us
  Pallas kernels  20.6 us (91%)
  local copies, waits for them, and re-layouts  1.54 us (7%)
    pallas_call x1, Pallas kernels, per_device(): pl.pallas_call(functools.partial(kernel, counts), out_shape=jax.ShapeDtyp...  20.6 us
    unnamed x1, local copies, waits for them, and re-layouts  1.54 us

profile of v2, /device:TPU:1, one launch (start us, length us, event | category | flops | bytes accessed | tf_op | source)
XLA Modules:
  0.0 22.2 jit_solution(5655238382717279701)
XLA Ops:
  0.0 20.6 %shard_map.55 = f32[3,8,8,128]{3,2,1,0:T(8,128)} custom-call(f32[3,8,8,128]{3,2,1,0:T(8,128)} %start.1, f32[3,8,8,128]{3,2,1,0:T(8,128)} %inertial.1, s32[8,8,128]{2,1,0:T(8,128)} %material.1, s32[8,8,128]{2,1,0:T(8,128)} %pinned.1, f32[8]{0:T(128)} %stiff.1), custom_call_target="tpu_custom_call" | custom-call | tf_op jit(solution)/shard_map/pallas_call | solution.py:522
  20.6 1.5 %copy.7 = f32[3,8,8,128]{3,2,1,0:T(8,128)} copy(f32[3,8,8,128]{3,2,1,0:T(8,128)} %shard_map.55) | data formatting | bytes 196608

commit v3 on v2

--- a/solution.py
+++ b/solution.py
@@ -143,7 +143,7 @@
 
 def kernel(
     counts, start, inertial, material, pinned, stiff, out,
-    first, mat, pins, ext, pk, rz, strip, sprev, srate, zin, prev, rate, terms, press, done,
+    first, mat, pins, ext, pk, rz, strip, sprev, srate, zin, prev, rate, terms, press,
     send_sem, recv_sem, load_sem,
 ):
     size_x, size_y, size_z = material.shape
@@ -350,7 +350,7 @@
             hi = hi - 3
         loop(lo, hi, voxels, 2)
 
-    loop(HALO, top, setup, 4)
+    loop(HALO, top, setup, SLOT)
     all_voxels(HALO, top - 1)
 
     for k, offset in enumerate(AROUND):
@@ -394,28 +394,32 @@
         for s in range(2):
             low, high = [], []
             for c in range(3):
-                t = make_terms(strip[s, c])
-                low.append(t)
-                high.append([xup(v) for v in t])
+                u = strip[s, c] * 0.25
+                low.append(node_terms(u, zup(u), up))
+                high.append(node_terms(xup(u), pltpu.roll(u, size_z - SLOT - 1, 1), up))
             made.append(stress(stretch(low, high), strip[s, WEIGHT]))
         for c in range(3):
-            sums, fresh = [], []
+            fresh = []
             for s in range(2):
-                mine = made[s][3 * c : 3 * c + 3]
-                minus, plus = node_sums([xdown(v) for v in mine], mine, down)
-                sums.append((minus, plus))
-                if step < ITERS - 1:
+                a, b, e = made[s][3 * c : 3 * c + 3]
+                both, less = a + b, a - b
+                e = e + down(e)
+                here, before = down(-less) - both, less + down(both)
+                last = step == ITERS - 1
+                if not last:
                     u = strip[s, c]
+                    f = (here - e) + xdown(before - e)
+                    f = f + (zdown(here + e) + pltpu.roll(before + e, SLOT + 1, 1))
                     fresh.append(advance(
-                        u, lambda: sprev[s, c], strip[s, INERT + c], srate[s],
-                        minus + zdown(plus), omegas[step],
+                        u, lambda: sprev[s, c], strip[s, INERT + c], srate[s], f, omegas[step]
                     ))
                     sprev[s, c] = u
                     strip[s, c] = fresh[s]
-            if step < ITERS - 1:
-                zin[step, c] = bring(*fresh)
-            else:
-                zin[step, c] = bring(zdown(sums[0][1]), sums[1][0])
+                elif s == 0:
+                    fresh.append(zdown(here + e) + pltpu.roll(before + e, SLOT + 1, 1))
+                else:
+                    fresh.append((here - e) + xdown(before - e))
+            zin[step, c] = bring(*fresh)
 
     for step in range(ITERS):
         strips(step)
@@ -479,7 +483,7 @@
                 made.append((x, c, u, fresh))
         if last:
             for x, c, _, fresh in made:
-                done[c, x - HALO] = fresh[0:size_y]
+                out[c, x - HALO] = fresh[0:size_y]
             return
         later = [(x, c, make_terms(fresh)) for x, c, _, fresh in made]
         for x, c, u, fresh in made:
@@ -493,14 +497,9 @@
         if step:
             all_voxels(step, planes - 1 - step)
         if step < ITERS - 1:
-            loop(step + 1, planes - 1 - step, functools.partial(nodes, step))
-
-    stores = []
-    for h in range(2):
-        loop(HALO * (h + 1), HALO * (h + 2), functools.partial(nodes, ITERS - 1), 4)
-        span = pl.ds(HALO * h, HALO)
-        stores.append(pltpu.make_async_copy(done.at[:, span], out.at[:, span], load_sem.at[h]))
-        stores[h].start()
+            loop(step + 1, planes - 1 - step, functools.partial(nodes, step), SLOT - 1 - step)
+
+    loop(HALO, top, functools.partial(nodes, ITERS - 1), HALO)
 
     for axis in range(2):
         sent_face(axis, 1)
@@ -508,8 +507,6 @@
         when(exists(offset), lambda k=k: piece(k).wait_send())
     for dx, dy in DIAGONAL:
         when(exists((dx, dy)), lambda dx=dx, dy=dy: corner(dx, dy, 1).wait_send())
-    for copy in stores:
-        copy.wait()
 
 
 def per_device(counts, start_disp, inertial, material, pinned, stiffness):
@@ -521,9 +518,9 @@
     i32 = lambda *shape: pltpu.VMEM(shape, jnp.int32)
     return pl.pallas_call(
         functools.partial(kernel, counts),
-        out_shape=jax.ShapeDtypeStruct(start_disp.shape, jnp.float32),
+        out_shape=pltpu.VMEM(start_disp.shape, jnp.float32),
         in_specs=[hbm, hbm, hbm, hbm, pl.BlockSpec(memory_space=pltpu.SMEM)],
-        out_specs=hbm,
+        out_specs=pl.BlockSpec(memory_space=pltpu.VMEM),
         scratch_shapes=[
             f32(3, size_x, size_y, size_z),
             i32(size_x, size_y, size_z),
@@ -539,7 +536,6 @@
             f32(planes, rows, size_z),
             f32(planes, 9, rows, size_z),
             f32(planes, 9, rows, size_z),
-            f32(3, size_x, size_y, size_z),
             pltpu.SemaphoreType.DMA((COPIES,)),
             pltpu.SemaphoreType.DMA((COPIES,)),
             pltpu.SemaphoreType.DMA((4,)),

time: 22.6 us -> 19.4 us (0.86)
  the two profiles are of different devices: /device:TPU:1 before, /device:TPU:0 now
where the time goes in v3:
time: 19.4 us; the launch traced here: 19.3 us
  Pallas kernels  18.6 us (96%)
  local copies, waits for them, and re-layouts  0.64 us (3%)
    pallas_call x1, Pallas kernels, per_device(): pl.pallas_call(functools.partial(kernel, counts), out_shape=pltpu.VMEM(st...  18.6 us
    unnamed x1, local copies, waits for them, and re-layouts  0.64 us

profile of v3, /device:TPU:0, one launch (start us, length us, event | category | flops | bytes accessed | tf_op | source)
XLA Modules:
  0.0 19.3 jit_solution(2479886049496279732)
XLA Ops:
  0.0 18.6 %shard_map.55 = f32[3,8,8,128]{3,2,1,0:T(8,128)S(1)} custom-call(f32[3,8,8,128]{3,2,1,0:T(8,128)} %start.1, f32[3,8,8,128]{3,2,1,0:T(8,128)} %inertial.1, s32[8,8,128]{2,1,0:T(8,128)} %material.1, s32[8,8,128]{2,1,0:T(8,128)} %pinned.1, f32[8]{0:T(128)} %stiff.1), custom_call_target="tpu_custom_call" | custom-call | tf_op jit(solution)/shard_map/pallas_call | solution.py:519
  18.6 0.6 %copy.7 = f32[3,8,8,128]{3,2,1,0:T(8,128)} copy(f32[3,8,8,128]{3,2,1,0:T(8,128)S(1)} %shard_map.55) | data formatting | bytes 196608

commit v4 on v3

--- a/solution.py
+++ b/solution.py
@@ -22,9 +22,7 @@
 AXES = ("gx", "gy", "gz")
 AROUND = tuple(o for o in itertools.product((-1, 0, 1), repeat=3) if any(o))
 DIAGONAL = tuple(itertools.product((-1, 1), repeat=2))
-FACES = len(AROUND)
-CORNERS = FACES + 8
-COPIES = CORNERS + 8
+SENT, PIECES, HALVES, NEAR, FAR = 0, 1, 2, 4, 5
 
 
 def loop(lo, hi, body, unroll=2):
@@ -142,9 +140,9 @@
 
 
 def kernel(
-    counts, start, inertial, material, pinned, stiff, out,
-    first, mat, pins, ext, pk, rz, strip, sprev, srate, zin, prev, rate, terms, press,
-    send_sem, recv_sem, load_sem,
+    counts, start, inertial, material, pinned, stiffness, out,
+    stiff, first, mat, pins, ext, pk, rz, strip, sprev, srate, zin, prev, rate, terms, press,
+    spare, copy_sem, load_sem,
 ):
     size_x, size_y, size_z = material.shape
     top = HALO + size_x
@@ -156,9 +154,10 @@
 
     loads = [
         pltpu.make_async_copy(pinned, pins, load_sem.at[0]),
-        pltpu.make_async_copy(material, mat, load_sem.at[1]),
-        pltpu.make_async_copy(inertial, ext.at[pl.ds(INERT, 3), own_x, own_y], load_sem.at[2]),
-        pltpu.make_async_copy(start, first, load_sem.at[3]),
+        pltpu.make_async_copy(material, mat, load_sem.at[0]),
+        pltpu.make_async_copy(inertial, ext.at[pl.ds(INERT, 3), own_x, own_y], load_sem.at[0]),
+        pltpu.make_async_copy(start, first, load_sem.at[0]),
+        pltpu.make_async_copy(stiffness, stiff, load_sem.at[1]),
     ]
     for copy in loads:
         copy.start()
@@ -173,9 +172,6 @@
     def peer(offset):
         return {AXES[i]: here[i] + o for i, o in enumerate(offset) if o}
 
-    def back(offset):
-        return tuple(-o for o in offset)
-
     blank = jnp.zeros((size_y, size_z), jnp.float32)
 
     def clear(xs, spots):
@@ -184,12 +180,15 @@
                 for spot in spots:
                     ext[a, x, spot * size_y : (spot + 1) * size_y] = blank
 
+    def slot(z, spot, g, group):
+        return 2 * (4 * (2 * z + spot) + g) + group
+
     for z in range(3):
-        for group in range(2):
+        for spot in range(2):
             for g in range(4):
-                for spot in range(2):
-                    if (z, spot) != (1, 0) or g in (0, 3):
-                        rz[z, group, g, spot * size_y : (spot + 1) * size_y] = blank
+                if (z, spot) != (1, 0) or g in (0, 3):
+                    for group in range(2):
+                        rz[slot(z, spot, g, group)] = blank
     loop(0, HALO, lambda xs: clear(xs, (0, 1)), 2)
     loop(HALO, top, lambda xs: clear(xs, (1,)), 4)
     loop(top, planes, lambda xs: clear(xs, (0, 1)), 2)
@@ -205,11 +204,12 @@
     sub = lax.broadcasted_iota(jnp.int32, (size_y, size_z), 0)
     lane = lax.broadcasted_iota(jnp.int32, (size_y, size_z), 1)
     inside = ((sub < size_y - 1) | has[1][1]) & ((lane < size_z - 1) | has[2][1])
+    block = size_z // 4
+
+    part = spare.at[pl.ds(0, 8 * size_x)]
+    pltpu.make_async_copy(part, part, load_sem.at[0]).wait()
+    loads[-1].wait()
     quarter = [stiff[i] * 0.25 for i in range(MATS)]
-    block = size_z // 4
-
-    for copy in loads:
-        copy.wait()
 
     for h in range(2):
         packed = [blank, blank]
@@ -232,12 +232,12 @@
                 mine = (lane >= spot) & (lane < spot + SLOT)
                 packed[a // SPAN] = jnp.where(mine, moved, packed[a // SPAN])
         for group in range(2):
-            pk[group, h] = packed[group]
-            rz[1, group, 1 + h, 0:size_y] = packed[group]
+            pk[2 * h + group] = packed[group]
+            rz[slot(1, 0, 1 + h, group)] = packed[group]
 
     def remote(src, dst, k, offset):
         return pltpu.make_async_remote_copy(
-            src_ref=src, dst_ref=dst, send_sem=send_sem.at[k], recv_sem=recv_sem.at[k],
+            src_ref=src, dst_ref=dst, send_sem=copy_sem.at[SENT], recv_sem=copy_sem.at[k],
             device_id=peer(offset), device_id_type=pl.DeviceIdType.MESH,
         )
 
@@ -255,12 +255,12 @@
             return pl.ds(top - depth, depth), pl.ds(HALO - depth, depth)
         return pl.ds(HALO, depth), pl.ds(top, depth)
 
-    def piece(k):
-        dx, dy, dz = AROUND[k]
-        parts = {0: (pl.ds(0, 2), pl.ds(1, 2)), 1: (pl.ds(1, 1), pl.ds(0, 1)), -1: (pl.ds(0, 1), pl.ds(3, 1))}
-        h, g = parts[dx]
-        r, to = row_spans(dy, HALO)
-        return remote(pk.at[:, h, r], rz.at[1 - dz, :, g, to], k, AROUND[k])
+    def piece(offset):
+        dx, dy, dz = offset
+        h, g, n = {0: (0, 1, 2), 1: (1, 0, 1), -1: (0, 3, 1)}[dx]
+        r, _ = row_spans(dy, HALO)
+        to = slot(1 - dz, abs(dy), g, 0)
+        return remote(pk.at[pl.ds(2 * h, 2 * n), r], rz.at[pl.ds(to, 2 * n), r], PIECES, offset)
 
     depths = (HALO, HALO - 1)
     sides = (-1, 1)
@@ -270,17 +270,21 @@
         x, x_to = plane_spans(offset[0], depths[group])
         y, y_to = row_spans(offset[1], depths[group])
         span = pl.ds(SPAN * group, SPAN)
-        k = FACES + 4 * axis + 2 * group + (side > 0)
-        return remote(ext.at[span, x, y], ext.at[span, x_to, y_to], k, offset)
+        return remote(ext.at[span, x, y], ext.at[span, x_to, y_to], (NEAR, FAR)[group], offset)
+
+    def half(side, part):
+        x = pl.ds(HALO * (1 + part), HALO)
+        y, y_to = row_spans(side, HALO)
+        span = pl.ds(0, SPAN)
+        return remote(ext.at[span, x, y], ext.at[span, x, y_to], HALVES + part, (0, side, 0))
 
     def corner(dx, dy, group):
         x, x_to = plane_spans(dx, depths[group])
-        y, y_to = row_spans(dy, depths[group])
+        y, y_to = row_spans(dy, HALO)
         span = pl.ds(SPAN * group, SPAN)
-        k = CORNERS + 4 * group + 2 * (dx > 0) + (dy > 0)
         if group == 0:
-            return remote(ext.at[span, x, y_to], ext.at[span, x_to, y_to], k, (dx, 0, 0))
-        return remote(ext.at[span, x, y], ext.at[span, x_to, y_to], k, (dx, dy, 0))
+            return remote(ext.at[span, x, y_to], ext.at[span, x_to, y_to], NEAR, (dx, 0, 0))
+        return remote(ext.at[span, x, y], ext.at[span, x_to, y_to], FAR, (dx, dy, 0))
 
     def when(condition, action):
         pl.when(condition)(action)
@@ -289,31 +293,49 @@
         for side in sides:
             when(has[axis][side], lambda side=side: face(axis, side, group).start())
 
-    def get_face(axis, group):
+    near = lambda nx, ny, nz: 16 * nx + 8 * nx * ny
+    far = lambda nx, ny, nz: 12 * nx + 12 * ny + 6 * nx * ny
+    halves = lambda nx, ny, nz: 8 * ny
+    pieces = lambda nx, ny, nz: (2 + nx) * (2 + ny) * (1 + nz) - 4
+
+    def sent(*n):
+        return pieces(*n) + 2 * halves(*n) + near(*n) + far(*n)
+
+    beside = [has[i][-1].astype(jnp.int32) + has[i][1].astype(jnp.int32) for i in range(3)]
+    choices = list(itertools.product(*[sorted({min(n - 1, 1), min(n - 1, 2)}) for n in counts]))
+
+    def drain(k, tiles):
+        for sizes in sorted({tiles(*n) for n in choices}):
+            if not sizes:
+                continue
+            found = None
+            for n in choices:
+                if tiles(*n) == sizes:
+                    same = (beside[0] == n[0]) & (beside[1] == n[1]) & (beside[2] == n[2])
+                    found = same if found is None else found | same
+
+            @pl.when(found)
+            def _(sizes=sizes):
+                part = spare.at[pl.ds(0, sizes)]
+                pltpu.make_async_copy(part, part, copy_sem.at[k]).wait()
+
+    pl.semaphore_wait(barrier, (1 + beside[0]) * (1 + beside[1]) * (1 + beside[2]) - 1)
+
+    for part in range(2):
         for side in sides:
-            when(has[axis][-side], lambda side=side: face(axis, side, group).wait_recv())
-
-    def sent_face(axis, group):
-        for side in sides:
-            when(has[axis][side], lambda side=side: face(axis, side, group).wait_send())
-
-    n = 1
-    for i in range(3):
-        n = n * (1 + has[i][-1].astype(jnp.int32) + has[i][1].astype(jnp.int32))
-    pl.semaphore_wait(barrier, n - 1)
-
-    send_face(1, 0)
+            when(has[1][side], lambda side=side, part=part: half(side, part).start())
     send_face(0, 0)
-    for k, offset in enumerate(AROUND):
-        when(exists(offset), lambda k=k: piece(k).start())
+    for offset in AROUND:
+        when(exists(offset), lambda offset=offset: piece(offset).start())
     send_face(1, 1)
     send_face(0, 1)
+
+    for part, dx in enumerate(sides):
+        drain(HALVES + part, halves)
+        for dy in sides:
+            when(has[0][dx] & has[1][-dy], lambda dx=dx, dy=dy: corner(dx, dy, 0).start())
     for dx, dy in DIAGONAL:
         when(exists((dx, dy)), lambda dx=dx, dy=dy: corner(dx, dy, 1).start())
-
-    get_face(1, 0)
-    for dx, dy in DIAGONAL:
-        when(has[0][dx] & has[1][-dy], lambda dx=dx, dy=dy: corner(dx, dy, 0).start())
 
     wide = lax.broadcasted_iota(jnp.int32, (rows, size_z), 1)
     edge = (wide == 0) | (wide == size_z - 1)
@@ -350,26 +372,40 @@
             hi = hi - 3
         loop(lo, hi, voxels, 2)
 
+    def weigh(xs):
+        made = []
+        for x in xs:
+            w = ext[WEIGHT, x - 1] + ext[WEIGHT, x]
+            w = w + down(w)
+            made.append((x, relax / (1.0 + 0.75 * (w + zdown(w)))))
+        for x, value in made:
+            rate[x] = value
+
+    own = list(range(HALO, top))
+    weigh(own[1:])
     loop(HALO, top, setup, SLOT)
     all_voxels(HALO, top - 1)
 
-    for k, offset in enumerate(AROUND):
-        when(exists(back(offset)), lambda k=k: piece(k).wait_recv())
-
-    late = lax.rem(wide, SLOT) >= HALO
+    drain(PIECES, pieces)
+
+    late = lax.rem(lane, SLOT) >= HALO
     for group in range(2):
         for s in range(2):
-            parts = [
-                jnp.where(late, rz[s + 1, group, g], rz[s, group, g]) for g in range(4)
-            ]
-            for j in range(SPAN):
-                value = None
-                for g in range(4):
-                    moved = parts[g]
-                    if g != j:
-                        moved = pltpu.roll(moved, (block * (g - j)) % size_z, 1)
-                    value = moved if g == 0 else jnp.where(wide >= block * g, moved, value)
-                strip[s, SPAN * group + j] = value
+            for spot in range(2):
+                parts = [
+                    jnp.where(
+                        late, rz[slot(s + 1, spot, g, group)], rz[slot(s, spot, g, group)]
+                    )
+                    for g in range(4)
+                ]
+                for j in range(SPAN):
+                    value = None
+                    for g in range(4):
+                        moved = parts[g]
+                        if g != j:
+                            moved = pltpu.roll(moved, (block * (g - j)) % size_z, 1)
+                        value = moved if g == 0 else jnp.where(lane >= block * g, moved, value)
+                    strip[s, SPAN * group + j, size_y * spot : size_y * (spot + 1)] = value
 
     def speed(total, pin):
         return jnp.where(pin > 0.0, 0.0, relax / (1.0 + 0.75 * total))
@@ -421,26 +457,18 @@
                     fresh.append((here - e) + xdown(before - e))
             zin[step, c] = bring(*fresh)
 
-    for step in range(ITERS):
+    for step in range(ITERS - 1):
         strips(step)
 
-    get_face(0, 0)
-    for dx, dy in DIAGONAL:
-        when(has[0][-dx] & has[1][-dy], lambda dx=dx, dy=dy: corner(dx, dy, 0).wait_recv())
-    loop(0, HALO, setup, 4)
-    loop(top, planes, setup, 4)
-    all_voxels(0, HALO)
-    all_voxels(top - 1, planes - 1)
-
-    get_face(1, 1)
-    get_face(0, 1)
-    for dx, dy in DIAGONAL:
-        when(has[0][-dx] & has[1][-dy], lambda dx=dx, dy=dy: corner(dx, dy, 1).wait_recv())
-
-    for axis in range(2):
-        sent_face(axis, 0)
-    for dx, dy in DIAGONAL:
-        when(has[0][dx] & has[1][-dy], lambda dx=dx, dy=dy: corner(dx, dy, 0).wait_send())
+    drain(NEAR, near)
+    weigh([x for x in range(1, planes - 1) if x not in own[1:]])
+    setup([x for x in range(planes) if x not in own])
+    strips(ITERS - 1)
+    for x in (0, 2, top - 1, top + 1):
+        voxels([x, x + 1])
+
+    drain(FAR, far)
+    drain(SENT, sent)
 
     def place(value, x):
         return pltpu.roll(value, size_z - SLOT * x, 1)
@@ -459,10 +487,15 @@
     loop(1, planes - 1, weigh, (planes - 2) // 2)
 
     def nodes(step, xs):
-        made = []
+        made, masked = [], []
         last = step == ITERS - 1
         for x in xs:
             r = rate[x]
+            if step == 0:
+                r = jnp.where(ext[PIN, x] > 0.0, 0.0, r)
+                masked.append((x, r))
+            if last:
+                r = jnp.where(wide == 0, pltpu.roll(srate[0], 2 * size_z - HALO - SLOT * x, 1), r)
             for c in range(3):
                 minus, plus = node_sums(
                     [press[x - 1, 3 * c + k] for k in range(3)],
@@ -486,6 +519,8 @@
                 out[c, x - HALO] = fresh[0:size_y]
             return
         later = [(x, c, make_terms(fresh)) for x, c, _, fresh in made]
+        for x, r in masked:
+            rate[x] = r
         for x, c, u, fresh in made:
             prev[c, x] = u
             ext[c, x] = fresh
@@ -500,13 +535,6 @@
             loop(step + 1, planes - 1 - step, functools.partial(nodes, step), SLOT - 1 - step)
 
     loop(HALO, top, functools.partial(nodes, ITERS - 1), HALO)
-
-    for axis in range(2):
-        sent_face(axis, 1)
-    for k, offset in enumerate(AROUND):
-        when(exists(offset), lambda k=k: piece(k).wait_send())
-    for dx, dy in DIAGONAL:
-        when(exists((dx, dy)), lambda dx=dx, dy=dy: corner(dx, dy, 1).wait_send())
 
 
 def per_device(counts, start_disp, inertial, material, pinned, stiffness):
@@ -519,15 +547,16 @@
     return pl.pallas_call(
         functools.partial(kernel, counts),
         out_shape=pltpu.VMEM(start_disp.shape, jnp.float32),
-        in_specs=[hbm, hbm, hbm, hbm, pl.BlockSpec(memory_space=pltpu.SMEM)],
+        in_specs=[hbm] * 5,
         out_specs=pl.BlockSpec(memory_space=pltpu.VMEM),
         scratch_shapes=[
+            pltpu.SMEM(stiffness.shape, jnp.float32),
             f32(3, size_x, size_y, size_z),
             i32(size_x, size_y, size_z),
             i32(size_x, size_y, size_z),
             f32(NARR, planes, rows, size_z),
-            f32(2, 2, size_y, size_z),
-            f32(3, 2, 4, rows, size_z),
+            f32(4, size_y, size_z),
+            f32(48, size_y, size_z),
             f32(2, NARR, rows, size_z),
             f32(2, 3, rows, size_z),
             f32(2, rows, size_z),
@@ -536,9 +565,9 @@
             f32(planes, rows, size_z),
             f32(planes, 9, rows, size_z),
             f32(planes, 9, rows, size_z),
-            pltpu.SemaphoreType.DMA((COPIES,)),
-            pltpu.SemaphoreType.DMA((COPIES,)),
-            pltpu.SemaphoreType.DMA((4,)),
+            f32(256, size_y, size_z),
+            pltpu.SemaphoreType.DMA((FAR + 1,)),
+            pltpu.SemaphoreType.DMA((2,)),
         ],
         compiler_params=pltpu.CompilerParams(collective_id=0, has_side_effects=True),
     )(start_disp, inertial, material, pinned, stiffness)

time: 19.4 us -> 17.8 us (0.918)
  the two profiles are of different devices: /device:TPU:0 before, /device:TPU:1 now
where the time goes in v4:
time: 17.8 us; the launch traced here: 17.7 us
  Pallas kernels  17 us (96%)
  local copies, waits for them, and re-layouts  0.64 us (4%)
    pallas_call x1, Pallas kernels, per_device(): pl.pallas_call(functools.partial(kernel, counts), out_shape=pltpu.VMEM(st...  17 us
    unnamed x1, local copies, waits for them, and re-layouts  0.64 us

profile of v4, /device:TPU:1, one launch (start us, length us, event | category | flops | bytes accessed | tf_op | source)
XLA Modules:
  0.0 17.7 jit_solution(11175528629440660067)
XLA Ops:
  0.0 17.0 %shard_map.55 = f32[3,8,8,128]{3,2,1,0:T(8,128)S(1)} custom-call(f32[3,8,8,128]{3,2,1,0:T(8,128)} %start.1, f32[3,8,8,128]{3,2,1,0:T(8,128)} %inertial.1, s32[8,8,128]{2,1,0:T(8,128)} %material.1, s32[8,8,128]{2,1,0:T(8,128)} %pinned.1, f32[8]{0:T(128)} %stiffness.1), custom_call_target="tpu_custom_call" | custom-call | tf_op jit(solution)/shard_map/pallas_call | solution.py:547
  17.0 0.6 %copy.7 = f32[3,8,8,128]{3,2,1,0:T(8,128)} copy(f32[3,8,8,128]{3,2,1,0:T(8,128)S(1)} %shard_map.55) | data formatting | bytes 196608

commit v5 on v4

--- a/solution.py
+++ b/solution.py
@@ -20,7 +20,9 @@
 SPAN = NARR // 2
 WEIGHT, INERT, PIN = 3, 4, 7
 AXES = ("gx", "gy", "gz")
-AROUND = tuple(o for o in itertools.product((-1, 0, 1), repeat=3) if any(o))
+AROUND = tuple(
+    o for n in (3, 2, 1) for o in itertools.product((-1, 0, 1), repeat=3) if sum(map(abs, o)) == n
+)
 DIAGONAL = tuple(itertools.product((-1, 1), repeat=2))
 SENT, PIECES, HALVES, NEAR, FAR = 0, 1, 2, 4, 5
 
@@ -70,14 +72,19 @@
     k11, k22, k33 = (s[i, i] - mean for i in range(3))
     k12, k13, k23 = s[0, 1], s[0, 2], s[1, 2]
     a11, a12, a13, a23 = k11 * k11, k12 * k12, k13 * k13, k23 * k23
-    b23, c23 = k22 * k33, k12 * k13
-    spread = a11 - b23 + a12 + (a13 + a23)
-    spread = jnp.maximum(spread * (1.0 / 3.0), 1e-30)
+    b11 = k22 * k33
+    spread = jnp.maximum((a11 - b11 + a12 + (a13 + a23)) * (1.0 / 3.0), 1e-30)
     rp = lax.rsqrt(spread)
     rp2 = rp * rp
-    det = k11 * (b23 - a23) - k22 * a13 + ((c23 + c23) * k23 - k33 * a12)
+    b11 = b11 - a23
+    b22 = k11 * k33 - a13
+    b33 = k11 * k22 - a12
+    b12 = k13 * k23 - k12 * k33
+    b13 = k12 * k23 - k13 * k22
+    b23 = k12 * k13 - k23 * k11
+    det = k11 * b11 + (k12 * b12 + k13 * b13)
     half = 0.5 + 0.25 * (det * rp * rp2)
-    half = jnp.minimum(jnp.maximum(half, 1e-12), 1.0)
+    half = jnp.maximum(half, 1e-12)
     root = half * lax.rsqrt(half)
     e = COSINE[-1]
     for a in COSINE[-2::-1]:
@@ -107,16 +114,16 @@
     q12 = (qs[0] - qs[1]) * r12
     q23 = (qs[1] - qs[2]) * r23
     c2 = (q12 - q23) * r13
-    c0 = (w - qs[0]) + (q12 * e - c2 * (e * x2))
+    c0 = ((w - qs[0]) - 3.0 * c2) + e * (q12 - c2 * x2)
     c1 = (c2 * x3 - q12) * rp
     c2 = c2 * rp2
     g = {
-        (0, 0): (c0 + c1 * k11) - c2 * (a11 + (a12 + a13)),
-        (1, 1): (c0 + c1 * k22) - c2 * (k22 * k22 + (a12 + a23)),
-        (2, 2): (c0 + c1 * k33) - c2 * (k33 * k33 + (a13 + a23)),
-        (0, 1): c1 * k12 - c2 * (k13 * k23 - k12 * k33),
-        (0, 2): c1 * k13 - c2 * (k12 * k23 - k13 * k22),
-        (1, 2): c1 * k23 - c2 * (c23 - k23 * k11),
+        (0, 0): (c0 + c1 * k11) - c2 * b11,
+        (1, 1): (c0 + c1 * k22) - c2 * b22,
+        (2, 2): (c0 + c1 * k33) - c2 * b33,
+        (0, 1): c1 * k12 - c2 * b12,
+        (0, 2): c1 * k13 - c2 * b13,
+        (1, 2): c1 * k23 - c2 * b23,
     }
     pick = lambda i, j: g[min(i, j), max(i, j)]
     return [
@@ -367,10 +374,8 @@
                 press[x, k] = p[k]
 
     def all_voxels(lo, hi):
-        if (hi - lo) % 2:
-            voxels([hi - 3, hi - 2, hi - 1])
-            hi = hi - 3
-        loop(lo, hi, voxels, 2)
+        for x in range(hi - 1, lo - 1, -1):
+            voxels([x])
 
     def weigh(xs):
         made = []
@@ -472,19 +477,6 @@
 
     def place(value, x):
         return pltpu.roll(value, size_z - SLOT * x, 1)
-
-    def weigh(xs):
-        made = []
-        for x in xs:
-            w = ext[WEIGHT, x - 1] + ext[WEIGHT, x]
-            w = w + down(w)
-            value = speed(w + zdown(w), ext[PIN, x])
-            low = pltpu.roll(srate[0], size_z - HALO - SLOT * x + size_z, 1)
-            made.append((x, jnp.where(wide == 0, low, value)))
-        for x, value in made:
-            rate[x] = value
-
-    loop(1, planes - 1, weigh, (planes - 2) // 2)
 
     def nodes(step, xs):
         made, masked = [], []
@@ -532,9 +524,9 @@
         if step:
             all_voxels(step, planes - 1 - step)
         if step < ITERS - 1:
-            loop(step + 1, planes - 1 - step, functools.partial(nodes, step), SLOT - 1 - step)
-
-    loop(HALO, top, functools.partial(nodes, ITERS - 1), HALO)
+            nodes(step, list(range(planes - 2 - step, step, -1)))
+
+    nodes(ITERS - 1, list(range(HALO, top)))
 
 
 def per_device(counts, start_disp, inertial, material, pinned, stiffness):

time: 17.8 us -> 16.7 us (0.938)
  Pallas kernels: 17 us -> 15.8 us
    pallas_call x1, Pallas kernels: 17 us -> 15.8 us  [per_device(): pl.pallas_call(functools.partial(kernel, counts), out_shape=pltpu.VMEM(st...]
where the time goes in v5:
time: 16.7 us; the launch traced here: 16.4 us
  Pallas kernels  15.8 us (95%)
  local copies, waits for them, and re-layouts  0.64 us (4%)
    pallas_call x1, Pallas kernels, per_device(): pl.pallas_call(functools.partial(kernel, counts), out_shape=pltpu.VMEM(st...  15.8 us
    unnamed x1, local copies, waits for them, and re-layouts  0.64 us

profile of v5, /device:TPU:1, one launch (start us, length us, event | category | flops | bytes accessed | tf_op | source)
XLA Modules:
  0.0 16.4 jit_solution(8291866821726062996)
XLA Ops:
  0.0 15.8 %shard_map.55 = f32[3,8,8,128]{3,2,1,0:T(8,128)S(1)} custom-call(f32[3,8,8,128]{3,2,1,0:T(8,128)} %start.1, f32[3,8,8,128]{3,2,1,0:T(8,128)} %inertial.1, s32[8,8,128]{2,1,0:T(8,128)} %material.1, s32[8,8,128]{2,1,0:T(8,128)} %pinned.1, f32[8]{0:T(128)} %stiffness.1), custom_call_target="tpu_custom_call" | custom-call | tf_op jit(solution)/shard_map/pallas_call | solution.py:539
  15.8 0.6 %copy.7 = f32[3,8,8,128]{3,2,1,0:T(8,128)} copy(f32[3,8,8,128]{3,2,1,0:T(8,128)S(1)} %shard_map.55) | data formatting | bytes 196608

commit v6 on v5

--- a/solution.py
+++ b/solution.py
@@ -148,7 +148,7 @@
 
 def kernel(
     counts, start, inertial, material, pinned, stiffness, out,
-    stiff, first, mat, pins, ext, pk, rz, strip, sprev, srate, zin, prev, rate, terms, press,
+    stiff, first, mat, pins, ext, pk, rz, strip, sprev, srate, zin, prev, rate, terms, press, edge_w,
     spare, copy_sem, load_sem,
 ):
     size_x, size_y, size_z = material.shape
@@ -357,21 +357,37 @@
         u = u * 0.25
         return node_terms(u, zup(u), up)
 
+    def line(x, k, n=rows):
+        return pl.ds((9 * x + k) * rows, n)
+
     def setup(xs):
         made = [(x, c, make_terms(ext[c, x])) for x in xs for c in range(3)]
         for x, c, three in made:
             for k in range(3):
-                terms[x, 3 * c + k] = three[k]
-
-    def voxels(xs):
-        made = []
+                terms[line(x, 3 * c + k)] = three[k]
+
+    def voxels(xs, n=rows):
         for x in xs:
-            low = [[terms[x, 3 * c + k] for k in range(3)] for c in range(3)]
-            high = [[terms[x + 1, 3 * c + k] for k in range(3)] for c in range(3)]
-            made.append((x, stress(stretch(low, high), ext[WEIGHT, x])))
-        for x, p in made:
+            low = [[terms[line(x, 3 * c + k, n)] for k in range(3)] for c in range(3)]
+            high = [[terms[line(x + 1, 3 * c + k, n)] for k in range(3)] for c in range(3)]
+            p = stress(stretch(low, high), ext[WEIGHT, x, 0:n])
             for k in range(9):
-                press[x, k] = p[k]
+                press[line(x, k, n)] = p[k]
+
+    def last_voxels():
+        lo = ITERS - 1
+
+        def across(x, k):
+            return pl.ds((9 * x + k + 1) * rows - 1, size_y, 9 * rows)
+
+        voxels([top - 1])
+        low = [[terms[across(lo, 3 * c + k)] for k in range(3)] for c in range(3)]
+        high = [[terms[across(lo + 1, 3 * c + k)] for k in range(3)] for c in range(3)]
+        p = stress(stretch(low, high), edge_w[...])
+        for k in range(9):
+            press[across(lo, k)] = p[k]
+        for x in range(top - 2, lo - 1, -1):
+            voxels([x], size_y)
 
     def all_voxels(lo, hi):
         for x in range(hi - 1, lo - 1, -1):
@@ -388,7 +404,7 @@
 
     own = list(range(HALO, top))
     weigh(own[1:])
-    loop(HALO, top, setup, SLOT)
+    setup(own)
     all_voxels(HALO, top - 1)
 
     drain(PIECES, pieces)
@@ -466,6 +482,8 @@
         strips(step)
 
     drain(NEAR, near)
+    for i in range(size_y):
+        edge_w[i : i + 1] = ext[WEIGHT, ITERS - 1 + i, rows - 1 : rows]
     weigh([x for x in range(1, planes - 1) if x not in own[1:]])
     setup([x for x in range(planes) if x not in own])
     strips(ITERS - 1)
@@ -490,8 +508,8 @@
                 r = jnp.where(wide == 0, pltpu.roll(srate[0], 2 * size_z - HALO - SLOT * x, 1), r)
             for c in range(3):
                 minus, plus = node_sums(
-                    [press[x - 1, 3 * c + k] for k in range(3)],
-                    [press[x, 3 * c + k] for k in range(3)],
+                    [press[line(x - 1, 3 * c + k)] for k in range(3)],
+                    [press[line(x, 3 * c + k)] for k in range(3)],
                     down,
                 )
                 plus = zdown(plus)
@@ -518,10 +536,12 @@
             ext[c, x] = fresh
         for x, c, three in later:
             for k in range(3):
-                terms[x, 3 * c + k] = three[k]
+                terms[line(x, 3 * c + k)] = three[k]
 
     for step in range(ITERS):
-        if step:
+        if step == ITERS - 1:
+            last_voxels()
+        elif step:
             all_voxels(step, planes - 1 - step)
         if step < ITERS - 1:
             nodes(step, list(range(planes - 2 - step, step, -1)))
@@ -555,8 +575,9 @@
             f32(ITERS, 3, rows, size_z),
             f32(3, planes, rows, size_z),
             f32(planes, rows, size_z),
-            f32(planes, 9, rows, size_z),
-            f32(planes, 9, rows, size_z),
+            f32(planes * 9 * rows, size_z),
+            f32(planes * 9 * rows, size_z),
+            f32(size_y, size_z),
             f32(256, size_y, size_z),
             pltpu.SemaphoreType.DMA((FAR + 1,)),
             pltpu.SemaphoreType.DMA((2,)),

time: 16.7 us -> 16.5 us (0.988)
  Pallas kernels: 15.8 us -> 15.6 us
    pallas_call x1, Pallas kernels: 15.8 us -> 15.6 us  [per_device(): pl.pallas_call(functools.partial(kernel, counts), out_shape=pltpu.VMEM(st...]
where the time goes in v6:
time: 16.5 us; the launch traced here: 16.2 us
  Pallas kernels  15.6 us (95%)
  local copies, waits for them, and re-layouts  0.64 us (4%)
    pallas_call x1, Pallas kernels, per_device(): pl.pallas_call(functools.partial(kernel, counts), out_shape=pltpu.VMEM(st...  15.6 us
    unnamed x1, local copies, waits for them, and re-layouts  0.64 us

profile of v6, /device:TPU:1, one launch (start us, length us, event | category | flops | bytes accessed | tf_op | source)
XLA Modules:
  0.0 16.2 jit_solution(9449210105090550017)
XLA Ops:
  0.0 15.6 %shard_map.55 = f32[3,8,8,128]{3,2,1,0:T(8,128)S(1)} custom-call(f32[3,8,8,128]{3,2,1,0:T(8,128)} %start.1, f32[3,8,8,128]{3,2,1,0:T(8,128)} %inertial.1, s32[8,8,128]{2,1,0:T(8,128)} %material.1, s32[8,8,128]{2,1,0:T(8,128)} %pinned.1, f32[8]{0:T(128)} %stiffness.1), custom_call_target="tpu_custom_call" | custom-call | tf_op jit(solution)/shard_map/pallas_call | solution.py:559
  15.6 0.6 %copy.7 = f32[3,8,8,128]{3,2,1,0:T(8,128)} copy(f32[3,8,8,128]{3,2,1,0:T(8,128)S(1)} %shard_map.55) | data formatting | bytes 196608

commit v7 on v6

--- a/solution.py
+++ b/solution.py
@@ -19,6 +19,7 @@
 NARR = 8
 SPAN = NARR // 2
 WEIGHT, INERT, PIN = 3, 4, 7
+FOLDED = ITERS - 3
 AXES = ("gx", "gy", "gz")
 AROUND = tuple(
     o for n in (3, 2, 1) for o in itertools.product((-1, 0, 1), repeat=3) if sum(map(abs, o)) == n
@@ -374,19 +375,25 @@
             for k in range(9):
                 press[line(x, k, n)] = p[k]
 
-    def last_voxels():
-        lo = ITERS - 1
-
-        def across(x, k):
-            return pl.ds((9 * x + k + 1) * rows - 1, size_y, 9 * rows)
-
-        voxels([top - 1])
-        low = [[terms[across(lo, 3 * c + k)] for k in range(3)] for c in range(3)]
-        high = [[terms[across(lo + 1, 3 * c + k)] for k in range(3)] for c in range(3)]
-        p = stress(stretch(low, high), edge_w[...])
-        for k in range(9):
-            press[across(lo, k)] = p[k]
-        for x in range(top - 2, lo - 1, -1):
+    def rim(step):
+        depth = ITERS - 1 - step
+        return [*range(rows - depth - 1, rows), *range(size_y, size_y + depth)]
+
+    rims = [(step, row) for step in range(FOLDED, ITERS) for row in rim(step)]
+
+    def folded_voxels(step):
+        def across(x, k, row):
+            return pl.ds((9 * x + k) * rows + row, size_y, 9 * rows)
+
+        for x in range(planes - 2 - step, step + size_y - 1, -1):
+            voxels([x])
+        for row in rim(step):
+            low = [[terms[across(step, 3 * c + k, row)] for k in range(3)] for c in range(3)]
+            high = [[terms[across(step + 1, 3 * c + k, row)] for k in range(3)] for c in range(3)]
+            p = stress(stretch(low, high), edge_w[rims.index((step, row))])
+            for k in range(9):
+                press[across(step, k, row)] = p[k]
+        for x in range(step + size_y - 1, step - 1, -1):
             voxels([x], size_y)
 
     def all_voxels(lo, hi):
@@ -482,8 +489,9 @@
         strips(step)
 
     drain(NEAR, near)
-    for i in range(size_y):
-        edge_w[i : i + 1] = ext[WEIGHT, ITERS - 1 + i, rows - 1 : rows]
+    for k, (step, row) in enumerate(rims):
+        for i in range(size_y):
+            edge_w[k, i : i + 1] = ext[WEIGHT, step + i, row : row + 1]
     weigh([x for x in range(1, planes - 1) if x not in own[1:]])
     setup([x for x in range(planes) if x not in own])
     strips(ITERS - 1)
@@ -539,8 +547,8 @@
                 terms[line(x, 3 * c + k)] = three[k]
 
     for step in range(ITERS):
-        if step == ITERS - 1:
-            last_voxels()
+        if step >= FOLDED:
+            folded_voxels(step)
         elif step:
             all_voxels(step, planes - 1 - step)
         if step < ITERS - 1:
@@ -577,7 +585,7 @@
             f32(planes, rows, size_z),
             f32(planes * 9 * rows, size_z),
             f32(planes * 9 * rows, size_z),
-            f32(size_y, size_z),
+            f32(SLOT * ITERS, size_y, size_z),
             f32(256, size_y, size_z),
             pltpu.SemaphoreType.DMA((FAR + 1,)),
             pltpu.SemaphoreType.DMA((2,)),

time: 16.5 us -> 16.4 us (level)
  no operation moved by 1% of the time
where the time goes in v7:
time: 16.4 us; the launch traced here: 16.2 us
  Pallas kernels  15.5 us (95%)
  local copies, waits for them, and re-layouts  0.64 us (4%)
    pallas_call x1, Pallas kernels, per_device(): pl.pallas_call(functools.partial(kernel, counts), out_shape=pltpu.VMEM(st...  15.5 us
    unnamed x1, local copies, waits for them, and re-layouts  0.64 us

profile of v7, /device:TPU:1, one launch (start us, length us, event | category | flops | bytes accessed | tf_op | source)
XLA Modules:
  0.0 16.2 jit_solution(4868718309280164187)
XLA Ops:
  0.0 15.5 %shard_map.55 = f32[3,8,8,128]{3,2,1,0:T(8,128)S(1)} custom-call(f32[3,8,8,128]{3,2,1,0:T(8,128)} %start.1, f32[3,8,8,128]{3,2,1,0:T(8,128)} %inertial.1, s32[8,8,128]{2,1,0:T(8,128)} %material.1, s32[8,8,128]{2,1,0:T(8,128)} %pinned.1, f32[8]{0:T(128)} %stiffness.1), custom_call_target="tpu_custom_call" | custom-call | tf_op jit(solution)/shard_map/pallas_call | solution.py:567
  15.5 0.6 %copy.7 = f32[3,8,8,128]{3,2,1,0:T(8,128)} copy(f32[3,8,8,128]{3,2,1,0:T(8,128)S(1)} %shard_map.55) | data formatting | bytes 196608
